TPU v7x, 256 devices: a whole 4x4x8 slice. The times are simulated.
256 devices in a mesh: dp: 8 (over y, core), vocab: 32 (over x, z).
Axes of the slice: x: 4, y: 4, z: 8, core: 2. Of those that a mesh axis runs over, the one named last changes fastest.
Arguments:
- teacher_hidden: bfloat16 [1024, 16384], P('dp', 'vocab'), may hold values from -120 to 120
- student_hidden: bfloat16 [1024, 4096], P('dp', 'vocab'), may hold values from -120 to 120
- teacher_weight: bfloat16 [16384, 65536], P('dp', 'vocab'), may hold values from -1 to 1
- student_weight: bfloat16 [4096, 65536], P('dp', 'vocab'), may hold values from -1 to 1
Outputs:
- kl: float32 [1024], P('dp')
- loss: float32 [], replicated
All inputs are finite; a program needn't handle non-finite values.
Results may differ from a plain program's by a relative error of at most 0.0003.
Values may be sent and summed in bfloat16 or wider, within the bound.
A program may use at most 128 MiB of HBM per device.

v0:
```python
import jax
import jax.numpy as jnp
from jax import lax
from jax.sharding import PartitionSpec as P


def joined_along(pieces, dim):
    pieces = jnp.moveaxis(pieces, 0, dim)
    shape = pieces.shape
    return pieces.reshape(*shape[:dim], shape[dim] * shape[dim + 1], *shape[dim + 2 :])


def gather_packed(arrays, axis, dims):
    vector = jnp.concatenate([a.reshape(-1) for a in arrays])
    lines, at, done = (lax.all_gather(vector, axis), 0, [])
    for a, dim in zip(arrays, dims):
        pieces = lines[:, at : at + a.size].reshape(-1, *a.shape)
        done.append(joined_along(pieces, dim))
        at += a.size
    return tuple(done)


def copy_for_each(x, axis):
    copies = jnp.broadcast_to(x, (lax.axis_size(axis), *x.shape))
    return lax.all_to_all(copies, axis, split_axis=0, concat_axis=0, tiled=True)


def collected_together(x, axis):
    leaves = jax.tree.leaves(x)
    sequence = sorted(range(len(leaves)), key=lambda k: -leaves[k].size)
    width = (1, *leaves[sequence[0]].shape)[-1]
    lines = [
        jnp.pad(leaves[k].reshape(-1), (0, -leaves[k].size % width)).reshape(-1, width)
        for k in sequence
    ]
    both, at, found = (copy_for_each(jnp.concatenate(lines), axis), 0, {})
    for k, line in zip(sequence, lines):
        piece = both[:, at : at + len(line)].reshape(len(both), -1)
        found[k] = piece[:, : leaves[k].size].reshape(-1, *leaves[k].shape)
        at += len(line)
    numbers = iter(range(len(leaves)))
    return jax.tree.map(lambda _: found[next(numbers)], x)


def combined_pairwise(pieces, combine):
    while len(jax.tree.leaves(pieces)[0]) > 1:
        pieces = jax.vmap(combine)(
            *(jax.tree.map(lambda part: part[side::2], pieces) for side in (0, 1))
        )
    return jax.tree.map(lambda part: part[0], pieces)


def combined_all(x, axis, combine):
    pieces = collected_together(x, axis)
    return combined_pairwise(pieces, combine)


def over_copies(x, axis):
    everything = copy_for_each(x, axis)
    return jnp.sum(everything, axis=0)


def merge_parts(earlier, later):
    teacher_top = jnp.maximum(earlier[0], later[0])
    early_teacher = jnp.exp(earlier[0] - teacher_top)
    late_teacher = jnp.exp(later[0] - teacher_top)
    student_top = jnp.maximum(earlier[3], later[3])
    early_student = jnp.exp(earlier[3] - student_top)
    late_student = jnp.exp(later[3] - student_top)
    return (
        teacher_top,
        earlier[1] * early_teacher + later[1] * late_teacher,
        earlier[2] * early_teacher + later[2] * late_teacher,
        student_top,
        earlier[4] * early_student + later[4] * late_student,
    )


def shards(teacher_hidden, student_hidden, teacher_weight, student_weight):
    teacher_full, student_full = gather_packed((teacher_hidden, student_hidden), "vocab", (1, 1))
    tok_rows = teacher_hidden.shape[0]
    teacher_cols = lax.all_to_all(teacher_full, "dp", split_axis=1, concat_axis=0, tiled=True)
    teacher_logit = lax.psum_scatter(
        jnp.dot(teacher_cols, teacher_weight, preferred_element_type=jnp.float32),
        "dp",
        scatter_dimension=0,
        tiled=True,
    )
    student_logit = jnp.dot(
        student_full,
        lax.all_gather(student_weight, "dp", axis=0, tiled=True),
        preferred_element_type=jnp.float32,
    )
    teacher_local = jnp.max(teacher_logit, axis=1)
    student_local = jnp.max(student_logit, axis=1)
    teacher_exp = jnp.exp(teacher_logit - teacher_local[:, None])
    local_parts = (
        teacher_local,
        jnp.sum(teacher_exp, axis=1),
        jnp.sum(teacher_exp * (teacher_logit - student_logit), axis=1),
        student_local,
        jnp.sum(jnp.exp(student_logit - student_local[:, None]), axis=1),
    )
    teacher_top, teacher_total, weighted, student_top, student_total = combined_all(
        local_parts, "vocab", merge_parts
    )
    teacher_lse = teacher_top + jnp.log(teacher_total)
    student_lse = student_top + jnp.log(student_total)
    kl = weighted / teacher_total - teacher_lse + student_lse
    group_sum = over_copies(jnp.sum(kl), "dp")
    loss = group_sum / (tok_rows * lax.axis_size("dp"))
    return (kl, loss)


def solution(mesh):
    in_specs = (P("dp", "vocab"), P("dp", "vocab"), P("dp", "vocab"), P("dp", "vocab"))
    out_specs = (P("dp"), P())
    return jax.shard_map(shards, mesh=mesh, in_specs=in_specs, out_specs=out_specs, check_vma=False)
```

profile of v0, /device:TPU:1, one launch (start us, length us, event | category | flops | bytes accessed | tf_op | source)
XLA Modules:
  0.0 331.4 jit_solution(3609465614383478665)
XLA Ops:
  7.2 1.0 copy.37
  8.2 1.4 pad_maximum_fusion
  9.7 0.7 all-gather.4.cloned.1.call-update
  10.4 85.7 %all-gather.6.cloned.1.call-done = bf16[2621440]{0:T(1024)(128)(2,1)} async-done(((bf16[81920]{0:T(1024)(128)(2,1)}), bf16[2621440]{0:T(1024)(128)(2,1)}) %all-gather.6.cloned.1.call-update) | async-done | bytes 5242896 | tf_op jit(solution)/shard_map/all_gather | solution.py:15
  96.1 6.4 %reshape.80 = bf16[32,81920]{1,0:T(8,128)(2,1)} reshape(bf16[2621440]{0:T(1024)(128)(2,1)} %all-gather.6.cloned.1.call-done) | data formatting | bytes 10485760 | tf_op jit(solution)/shard_map/all_gather | solution.py:15
  102.5 2.2 slice-done
  104.7 3.5 %copy.38 = bf16[4,8,128,512]{3,2,1,0:T(8,128)(2,1)} copy(bf16[4,8,128,512]{3,1,2,0:T(8,128)(2,1)S(1)} %bitcast.39) | data formatting | bytes 8388608
  108.2 6.6 %copy.24 = bf16[128,32,512]{0,2,1:T(8,128)(2,1)} copy(bf16[128,32,512]{2,0,1:T(8,128)(2,1)} %bitcast.40) | data formatting | bytes 8388608 | tf_op jit(solution)/shard_map/transpose | solution.py:8
  114.8 102.4 %all_to_all.30 = bf16[128,8,2048]{0,2,1:T(8,128)(2,1)} all-to-all(bf16[128,8,2048]{0,2,1:T(8,128)(2,1)} %bitcast.41), channel_id=1, replica_groups=mesh['dp'=8,'vocab'=32] {'dp'}, dimensions={1} | all-to-all | bytes 8388608 | tf_op jit(solution)/shard_map/all_to_all | solution.py:82
  217.3 6.6 %copy.25 = bf16[8,128,2048]{2,1,0:T(8,128)(2,1)} copy(bf16[8,128,2048]{1,2,0:T(8,128)(2,1)} %bitcast.42) | data formatting | bytes 8388608 | tf_op jit(solution)/shard_map/all_to_all | solution.py:82
  223.8 14.4 %fusion.7 = f32[1024,2048]{1,0:T(8,128)} fusion(bf16[1024,2048]{1,0:T(8,128)(2,1)} %bitcast.44, bf16[2048,2048]{1,0:T(8,128)(2,1)} %param.6), kind=kOutput, calls=%fused_computation.35 | convolution fusion | flops 8589934592 | bytes 20971520 | tf_op jit(solution)/shard_map/dot_general | solution.py:84
  238.3 1.3 slice_bitcast_fusion
  239.6 0.2 copy.39
  239.8 0.7 copy.26
  240.5 9.0 %fusion.6 = (f32[128]{0:T(128)S(1)}, f32[128,2048]{1,0:T(8,128)S(1)}) fusion(bf16[128,4096]{0,1:T(8,128)(2,1)S(1)} %bitcast.43, bf16[4096,2048]{1,0:T(8,128)(2,1)} %all-gather.4.cloned.1.call-done), kind=kOutput, calls=%fused_computation.34 | convolution fusion | flops 2147745792 | bytes 18874880 | tf_op jit(solution)/shard_map/dot_general | solution.py:89
  249.5 38.8 %reduce-scatter.2.cloned.1.call-done = f32[128,2048]{1,0:T(8,128)} async-done(((f32[1024,2048]{1,0:T(8,128)}), f32[128,2048]{1,0:T(8,128)}) %reduce-scatter.2.cloned.1.call-update) | async-done | bytes 1048592 | tf_op jit(solution)/shard_map/reduce_scatter | solution.py:83
  288.3 1.4 reduce_max.18
  289.7 1.8 multiply_reduce_fusion
  291.4 18.5 %all_to_all.31 = f32[32,5,128]{2,1,0:T(8,128)S(1)} all-to-all(f32[32,5,128]{2,1,0:T(8,128)S(1)} %broadcast_in_dim.8), channel_id=1, replica_groups=mesh['dp'=8,'vocab'=32] {'vocab'}, dimensions={0} | all-to-all | bytes 163840 | tf_op jit(solution)/shard_map/all_to_all | solution.py:25
  310.0 0.1 fusion.5
  310.9 1.1 fusion.4
  312.0 0.6 broadcast_in_dim.9
  312.7 9.8 %all_to_all.32 = f32[8,1,1]{2,1,0:T(1,128)S(1)} all-to-all(f32[8,1,1]{2,1,0:T(1,128)S(1)} %broadcast_in_dim.9), channel_id=1, replica_groups=mesh['dp'=8,'vocab'=32] {'dp'}, dimensions={0} | all-to-all | bytes 64 | tf_op jit(solution)/shard_map/all_to_all | solution.py:25
  322.5 0.6 reduce_sum.49
  (60 shorter events, 1.0 us)
Async XLA Ops:
  7.2 89.0 %all-gather.6.cloned.1.call-start = ((), (), s32[]{:S(2)}) async-start(), calls=%async_computation.6 | async-start | bytes 5406720 | tf_op jit(solution)/shard_map/all_gather | solution.py:15
  9.6 230.9 %all-gather.4.cloned.1.call-start = ((), (), s32[]{:S(2)}) async-start(), calls=%async_computation.5 | async-start | bytes 18874368 | tf_op jit(solution)/shard_map/all_gather | solution.py:91
  10.4 277.9 %reduce-scatter.2.cloned.1.call-start = ((), (), s32[]{:S(2)}) async-start(), calls=%async_computation.4 | async-start | bytes 9437184 | tf_op jit(solution)/shard_map/reduce_scatter | solution.py:83
  102.5 2.2 slice-start
Sparse Core Ops, SparseCore 0:
  10.5 85.5 all-gather.5
  98.0 132.9 all-gather.3
  238.4 49.8 reduce-scatter.1
where the time goes:
time: 332 us; the launch traced here: 331 us
  blocking collectives  131 us (39%)
  waiting for transfers between devices  125 us (38%)
  local copies, waits for them, and re-layouts  29.7 us (9%)
  matrix products  23.4 us (7%)
  between operations  15.7 us (5%)
  other arithmetic  6.42 us (2%)
    all_to_all x1, blocking collectives, shards(): lax.all_to_all(teacher_full, 'dp', split_axis=1, concat_axis=0, tiled=True)  102 us
    all_gather x1, waiting for transfers between devices, gather_packed(): lines, at, done = (lax.all_gather(vector, axis), 0, [])  85.7 us
    reduce_scatter x1, waiting for transfers between devices, shards(): lax.psum_scatter(jnp.dot(teacher_cols, teacher_weight, preferred_element_...  38.8 us
    all_to_all x2, blocking collectives, copy_for_each(): return lax.all_to_all(copies, axis, split_axis=0, concat_axis=0, tiled=True)  28.4 us
    dot_general x1, matrix products, shards(): jnp.dot(teacher_cols, teacher_weight, preferred_element_type=jnp.float32)  14.4 us
    dot_general x1, matrix products, shards(): jnp.dot(student_full, lax.all_gather(student_weight, 'dp', axis=0, tiled=...  8.96 us
    transpose x2, local copies, waits for them, and re-layouts, joined_along(): pieces = jnp.moveaxis(pieces, 0, dim)  7.28 us
  transfers between devices with their start and end apart: 3, of which 2 were waited for; matrix products, arithmetic and copies ran while one was open for 15% of the time, Pallas kernels for 0%

commit v1 on v0

v1 whole, which is shorter than its diff:
```python
import jax
import jax.numpy as jnp
from jax import lax
from jax.experimental import pallas as pl
from jax.experimental.pallas import tpu as pltpu
from jax.sharding import PartitionSpec as P

NX, NY, NZ = 4, 4, 8
TOK = 128
TF = 512
SF = 128
VB = 2048
CB = VB // NY
F32 = jnp.float32

OFFS = (0, -1, 1, -2, 2, -3, 3, 4)
STAGES = ((0, 128), (128, 256), (384, 128))
N_REMOTE = 100


def body(
    th, sh, tw, sw,
    kl_ref, loss_ref,
    tbuf, sbuf, twb, swb, swst, pbuf, ropp, rfin, slog, stat, st1, st2, st3, st4,
    ssem, rsem, lsem,
):
    dp = lax.axis_index("dp")
    v = lax.axis_index("vocab")
    y, c = lax.div(dp, 2), lax.rem(dp, 2)
    x, z = lax.div(v, NZ), lax.rem(v, NZ)
    o = 1 - c

    def dev(xx, yy, zz, cc):
        return (yy * 2 + cc, xx * NZ + zz)

    def xm(d):
        return lax.rem(x + (d + NX), NX)

    def ym(d):
        return lax.rem(y + (d + NY), NY)

    def zm(d):
        return lax.rem(z + (d + NZ), NZ)

    started = []
    count = [0]

    def copy_to(src, dst, device):
        i = count[0]
        count[0] += 1
        return pltpu.make_async_remote_copy(
            src_ref=src,
            dst_ref=dst,
            send_sem=ssem.at[i],
            recv_sem=rsem.at[i],
            device_id=device,
            device_id_type=pl.DeviceIdType.MESH,
        )

    def send(src, dst, device):
        d = copy_to(src, dst, device)
        d.start()
        started.append(d)
        return d

    tw_own = pltpu.make_async_copy(tw, twb.at[pl.ds(c * VB, VB), :], lsem.at[0])
    tw_own.start()
    sw_own = pltpu.make_async_copy(
        sw.at[:, :, pl.ds(y * CB, CB)], swb.at[pl.ds(c * 4, 4), pl.ds(y * SF, SF), :], lsem.at[1]
    )
    sw_own.start()
    sh_own = pltpu.make_async_copy(
        sh, sbuf.at[z, pl.ds(y * TOK, TOK), pl.ds(x * SF, SF)], lsem.at[2]
    )
    sh_own.start()

    def tshard(slot, zz, lo=0, n=TOK):
        return tbuf.at[pl.ds(slot * TOK + lo, n), pl.ds(zz * TF, TF)]

    th_own = pltpu.make_async_copy(th, tshard(0, z), lsem.at[3])

    @pl.when(x == y)
    def _():
        th_own.start()

    barrier = pltpu.get_barrier_semaphore()
    peers = [dev(xm(d), y, z, c) for d in range(1, NX)]
    peers += [dev(x, y, zm(d), c) for d in range(1, NZ)]
    peers += [(lax.rem(dp + d, 8), v) for d in range(1, 8)]
    for p in peers:
        pl.semaphore_signal(barrier, inc=1, device_id=p, device_id_type=pl.DeviceIdType.MESH)

    @pl.when(x != y)
    def _():
        pl.semaphore_signal(
            barrier, inc=1, device_id=dev(y, x, z, c), device_id_type=pl.DeviceIdType.MESH
        )
        pl.semaphore_wait(barrier, len(peers) + 1)

    @pl.when(x == y)
    def _():
        pl.semaphore_wait(barrier, len(peers))

    R, L = dev(xm(1), y, z, c), dev(xm(-1), y, z, c)
    U, D = dev(x, ym(1), z, c), dev(x, ym(-1), z, c)
    F, B = dev(x, y, zm(1), c), dev(x, y, zm(-1), c)
    mate = dev(x, y, z, o)

    th_move = copy_to(th, tshard(0, z), dev(y, x, z, c))

    @pl.when(x != y)
    def _():
        th_move.start()

    s_y = [
        send(
            sh,
            sbuf.at[z, pl.ds(y * TOK, TOK), pl.ds(x * SF, SF)],
            dev(x, ym(d), z, c),
        )
        for d in (1, -1, 2)
    ]

    opp = ym(2)
    sw_st_d = send(sw.at[pl.ds(0, 2), :, pl.ds(opp * CB, CB)], swst.at[0], D)
    sw_st_u = send(sw.at[pl.ds(2, 2), :, pl.ds(opp * CB, CB)], swst.at[1], U)
    here = swb.at[pl.ds(c * 4, 4), pl.ds(y * SF, SF), :]
    sw_u = send(sw.at[:, :, pl.ds(ym(1) * CB, CB)], here, U)
    sw_d = send(sw.at[:, :, pl.ds(ym(-1) * CB, CB)], here, D)

    def tw_part(k):
        rows = pl.ds(k * 512, 512)
        return send(tw.at[rows, :], twb.at[pl.ds(c * VB + k * 512, 512), :], mate)

    tw_in = [tw_part(0)]

    sh_own.wait()
    for d in s_y:
        d.wait_recv()

    def sblock(xx, lo=0, n=512):
        return sbuf.at[z, pl.ds(lo, n), pl.ds(xx * SF, SF)]

    sx_r = send(sblock(x), sblock(x), R)
    sx_l = send(sblock(x), sblock(x), L)

    @pl.when(x != y)
    def _():
        th_move.wait_recv()

    @pl.when(x == y)
    def _():
        th_own.wait()

    tx = {}

    def send_x(off):
        zz = zm(off)
        tx[1, off] = send(tshard(0, zz), tshard(1, zz), R)
        tx[2, off] = send(tshard(0, zz), tshard(2, zz), L)

    tz_f = send(tshard(0, z), tshard(0, z), F)
    tz_b = send(tshard(0, z), tshard(0, z), B)
    send_x(0)
    for k in (1, 2, 3):
        tw_in.append(tw_part(k))
        tz_f.wait_recv()
        if k < 3:
            nf = send(tshard(0, zm(-k)), tshard(0, zm(-k)), F)
        else:
            nf = send(tshard(0, zm(-k), 0, 64), tshard(0, zm(-k), 0, 64), F)
        tz_b.wait_recv()
        if k < 3:
            nb = send(tshard(0, zm(k)), tshard(0, zm(k)), B)
        else:
            nb = send(tshard(0, zm(k), 64, 64), tshard(0, zm(k), 64, 64), B)
        tz_f, tz_b = nf, nb
        send_x(-k)
        send_x(k)
        if k == 1:
            sx_r.wait_recv()
            sx_fr = send(sblock(xm(-1), 0, 256), sblock(xm(-1), 0, 256), R)
            sx_l.wait_recv()
            sx_fl = send(sblock(xm(1), 256, 256), sblock(xm(1), 256, 256), L)
        if k == 2:
            sw_st_d.wait_recv()
            src = ym(1)
            sw_fd = send(swst.at[0], swb.at[pl.ds(c * 4, 2), pl.ds(src * SF, SF), :], D)
            sw_st_u.wait_recv()
            src = ym(-1)
            sw_fu = send(swst.at[1], swb.at[pl.ds(c * 4 + 2, 2), pl.ds(src * SF, SF), :], U)
    tz_f.wait_recv()
    tz_b.wait_recv()
    send_x(4)

    sx_fr.wait_recv()
    sx_fl.wait_recv()

    def sz_block(zz, lo=0, n=512):
        return sbuf.at[zz, pl.ds(lo, n), :]

    sz = {}
    sz["f"] = send(sz_block(z), sz_block(z), F)
    sz["b"] = send(sz_block(z), sz_block(z), B)

    def sz_step(k):
        n, lo = (512, 0) if k < 3 else (256, 256)
        sz["f"].wait_recv()
        sz["f"] = send(sz_block(zm(-k), 0, n), sz_block(zm(-k), 0, n), F)
        sz["b"].wait_recv()
        sz["b"] = send(sz_block(zm(k), lo, n), sz_block(zm(k), lo, n), B)

    def forward_r(off):
        tx[1, off].wait_recv()
        zz = zm(off)
        tx[3, off] = send(tshard(1, zz), tshard(3, zz), R)

    def forward_l(off):
        tx[2, off].wait_recv()
        zz = zm(off)
        tx[3, off] = send(tshard(2, zz), tshard(3, zz), L)

    targets = (ym(2), ym(-1), ym(1), y)

    def product(stage, q0, q1):
        lo, m = STAGES[stage]

        def step(i, carry):
            q = lax.div(i, 2)
            h = lax.rem(i, 2)
            tgt = lax.rem(y + jnp.where(q == 0, 2, jnp.where(q == 1, 3, jnp.where(q == 2, 1, 0))), NY)
            cols = pl.ds(pl.multiple_of(tgt * CB + h * 256, 256), 256)
            pbuf[q, lo : lo + m, pl.ds(pl.multiple_of(h * 256, 256), 256)] = jnp.dot(
                tbuf[lo : lo + m, :], twb[:, cols], preferred_element_type=F32
            )
            return carry

        lax.fori_loop(2 * q0, 2 * q1, step, 0)

    rs = {}

    def halves(stage):
        lo, m = STAGES[stage]
        return pl.ds(lo, m // 2), pl.ds(lo + m // 2, m // 2)

    def send_opp(stage):
        a, b = halves(stage)
        rs[stage, "oa"] = send(pbuf.at[0, a, :], ropp.at[a, :], D)
        rs[stage, "ob"] = send(pbuf.at[0, b, :], ropp.at[b, :], U)

    def send_plain(stage):
        a, b = halves(stage)
        rs[stage, "pb"] = send(pbuf.at[1, b, :], rfin.at[0, b, :], D)
        rs[stage, "pa"] = send(pbuf.at[2, a, :], rfin.at[1, a, :], U)

    def send_sums(stage):
        a, b = halves(stage)
        lo, m = STAGES[stage]
        h = m // 2
        rs[stage, "oa"].wait_recv()
        pbuf[1, lo : lo + h, :] += ropp[lo : lo + h, :]
        rs[stage, "sa"] = send(pbuf.at[1, a, :], rfin.at[0, a, :], D)
        rs[stage, "ob"].wait_recv()
        pbuf[2, lo + h : lo + m, :] += ropp[lo + h : lo + m, :]
        rs[stage, "sb"] = send(pbuf.at[2, b, :], rfin.at[1, b, :], U)

    def teacher_stage(stage):
        product(stage, 0, 1)
        send_opp(stage)
        product(stage, 1, 4)
        send_plain(stage)

    for off in OFFS[:4]:
        forward_r(off)
    tw_own.wait()
    for d in tw_in:
        d.wait_recv()
    teacher_stage(0)
    for off in OFFS[4:]:
        forward_l(off)
    send_sums(0)
    sz_step(1)
    for off in OFFS[4:]:
        tx[1, off].wait_recv()
    for off in OFFS[:4]:
        tx[2, off].wait_recv()
    teacher_stage(1)

    sw_own.wait()
    sw_mate = []

    def to_mate(src, first, n):
        part = swb.at[pl.ds(c * 4 + first, n), pl.ds(src * SF, SF), :]
        sw_mate.append(send(part, part, mate))

    to_mate(y, 0, 4)
    sw_u.wait_recv()
    to_mate(ym(-1), 0, 4)
    sw_d.wait_recv()
    to_mate(ym(1), 0, 4)
    sw_fd.wait_recv()
    sw_fu.wait_recv()
    to_mate(ym(2), 0, 4)

    send_sums(1)
    sz_step(2)
    for off in OFFS:
        tx[3, off].wait_recv()
    teacher_stage(2)
    for d in sw_mate:
        d.wait_recv()
    send_sums(2)
    sz_step(3)

    def student(off_lo, off_hi, first):
        def step(i, carry):
            zz = lax.rem(z + i, NZ)
            part = jnp.dot(sbuf[zz], swb[zz], preferred_element_type=F32)
            slog[...] += part
            return carry

        if first:
            slog[...] = jnp.zeros_like(slog)
        lax.fori_loop(off_lo, off_hi, step, 0)

    student(5, 12, True)
    sz["f"].wait_recv()
    sz["b"].wait_recv()
    student(4, 5, False)

    for stage in range(3):
        for name in ("pb", "pa", "sa", "sb"):
            rs[stage, name].wait_recv()

    lane = lax.broadcasted_iota(jnp.int32, (TOK, 128), 1)

    def token_stats(slot, carry):
        group = lax.rem(x + jnp.where(slot == 1, 3, jnp.where(slot == 2, 1, jnp.where(slot == 3, 2, 0))), NX)
        rows = pl.ds(pl.multiple_of(slot * TOK, TOK), TOK)
        t = pbuf[3, rows, :] + rfin[0, rows, :] + rfin[1, rows, :]
        s = slog[pl.ds(pl.multiple_of(group * TOK, TOK), TOK), :]
        t_top = jnp.max(t, axis=1, keepdims=True)
        s_top = jnp.max(s, axis=1, keepdims=True)
        e = jnp.exp(t - t_top)
        t_sum = jnp.sum(e, axis=1, keepdims=True)
        w = jnp.sum(e * (t - s), axis=1, keepdims=True)
        s_sum = jnp.sum(jnp.exp(s - s_top), axis=1, keepdims=True)
        both = jnp.where(
            lane == 0, t_top,
            jnp.where(lane == 1, t_sum, jnp.where(lane == 2, w, jnp.where(lane == 3, s_top, s_sum))),
        )
        stat[group] = jnp.transpose(both)[:8, :]
        return carry

    lax.fori_loop(0, 4, token_stats, 0)

    def merged(ref, n):
        parts = [ref[k] for k in range(n)]
        t_top = parts[0][0:1]
        s_top = parts[0][3:4]
        for p in parts[1:]:
            t_top = jnp.maximum(t_top, p[0:1])
            s_top = jnp.maximum(s_top, p[3:4])
        t_sum = w = s_sum = jnp.zeros((1, 128), F32)
        for p in parts:
            a = jnp.exp(p[0:1] - t_top)
            b = jnp.exp(p[3:4] - s_top)
            t_sum += p[1:2] * a
            w += p[2:3] * a
            s_sum += p[4:5] * b
        return t_top, t_sum, w, s_top, s_sum

    def put(ref, k, rows):
        zero = jnp.zeros((3, 128), F32)
        ref[k] = jnp.concatenate([*rows, zero], axis=0)

    st1[y] = stat[y]
    got = [send(stat.at[ym(d)], st1.at[y], dev(x, ym(d), z, c)) for d in range(1, NY)]
    for d in got:
        d.wait_recv()
    put(st2, x, merged(st1, NY))
    got = [send(st2.at[x], st2.at[x], dev(xm(d), y, z, c)) for d in range(1, NX)]
    for d in got:
        d.wait_recv()
    put(st3, z, merged(st2, NX))
    got = [send(st3.at[z], st3.at[z], dev(x, y, zm(d), c)) for d in range(1, NZ)]
    for d in got:
        d.wait_recv()
    t_top, t_sum, w, s_top, s_sum = merged(st3, NZ)
    kl = w / t_sum - (t_top + jnp.log(t_sum)) + (s_top + jnp.log(s_sum))
    kl_ref[...] = kl
    st4[dp] = jnp.broadcast_to(jnp.sum(kl, axis=1, keepdims=True), (8, 128))
    got = [send(st4.at[dp], st4.at[dp], (lax.rem(dp + d, 8), v)) for d in range(1, 8)]
    for d in got:
        d.wait_recv()
    total = st4[0]
    for k in range(1, 8):
        total += st4[k]
    loss_ref[...] = total * (1.0 / (TOK * 8))

    for d in started:
        d.wait_send()

    @pl.when(x != y)
    def _():
        th_move.wait_send()

    assert count[0] == N_REMOTE, count[0]


def shards(th, sh, tw, sw):
    hbm = pl.BlockSpec(memory_space=pl.ANY)
    vmem = pl.BlockSpec(memory_space=pltpu.VMEM)
    bf16 = jnp.bfloat16
    kl, loss = pl.pallas_call(
        body,
        out_shape=(
            jax.ShapeDtypeStruct((1, TOK), F32),
            jax.ShapeDtypeStruct((8, 128), F32),
        ),
        in_specs=[hbm] * 4,
        out_specs=(vmem, vmem),
        scratch_shapes=[
            pltpu.VMEM((4 * TOK, NZ * TF), bf16),
            pltpu.VMEM((NZ, 4 * TOK, NX * SF), bf16),
            pltpu.VMEM((2 * VB, VB), bf16),
            pltpu.VMEM((NZ, NX * SF, CB), bf16),
            pltpu.VMEM((2, 2, SF, CB), bf16),
            pltpu.VMEM((4, 4 * TOK, CB), F32),
            pltpu.VMEM((4 * TOK, CB), F32),
            pltpu.VMEM((2, 4 * TOK, CB), F32),
            pltpu.VMEM((4 * TOK, CB), F32),
            pltpu.VMEM((NY, 8, 128), F32),
            pltpu.VMEM((NY, 8, 128), F32),
            pltpu.VMEM((NX, 8, 128), F32),
            pltpu.VMEM((NZ, 8, 128), F32),
            pltpu.VMEM((8, 8, 128), F32),
            pltpu.SemaphoreType.DMA((N_REMOTE,)),
            pltpu.SemaphoreType.DMA((N_REMOTE,)),
            pltpu.SemaphoreType.DMA((4,)),
        ],
        compiler_params=pltpu.CompilerParams(
            collective_id=0, has_side_effects=True, vmem_limit_bytes=60 * 1024 * 1024
        ),
        name="kl_all",
    )(th, sh, tw, sw.reshape(4, SF, VB))
    return (kl.reshape(TOK), loss[0, 0])


def solution(mesh):
    in_specs = (P("dp", "vocab"),) * 4
    return jax.shard_map(
        shards, mesh=mesh, in_specs=in_specs, out_specs=(P("dp"), P()), check_vma=False
    )
```

time: 332 us -> 103 us (0.31)
  blocking collectives: 131 us -> 0 us
  waiting for transfers between devices: 125 us -> 0 us
  Pallas kernels: 0 us -> 100 us
  local copies, waits for them, and re-layouts: 29.7 us -> 2.32 us
  matrix products: 23.4 us -> 0 us
  between operations: 15.7 us -> 0.64 us
  other arithmetic: 6.42 us -> 0 us
    all_to_all x3 -> x0, blocking collectives: 131 us -> none  [the longest x1 102 us: shards(): lax.all_to_all(teacher_full, 'dp', split_axis=1, concat_axis=0, tiled=True)]
    pallas_call x0 -> x1, Pallas kernels: none -> 100 us  [shards(): pl.pallas_call(body, out_shape=(jax.ShapeDtypeStruct((1, TOK), F32), jax....]
    all_gather x2 -> x0, waiting for transfers between devices: 85.7 us -> none  [the longest x1 85.7 us: gather_packed(): lines, at, done = (lax.all_gather(vector, axis), 0, [])]
    reduce_scatter x1 -> x0, waiting for transfers between devices: 38.8 us -> none  [shards(): lax.psum_scatter(jnp.dot(teacher_cols, teacher_weight, preferred_element_...]
    dot_general x2 -> x0, matrix products: 23.4 us -> none  [the longest x1 14.4 us: shards(): jnp.dot(teacher_cols, teacher_weight, preferred_element_type=jnp.float32)]
    transpose x2 -> x0, local copies, waits for them, and re-layouts: 7.28 us -> none  [joined_along(): pieces = jnp.moveaxis(pieces, 0, dim)]
    all_to_all x1 -> x0, local copies, waits for them, and re-layouts: 6.58 us -> none  [shards(): lax.all_to_all(teacher_full, 'dp', split_axis=1, concat_axis=0, tiled=True)]
    all_gather x1 -> x0, local copies, waits for them, and re-layouts: 6.39 us -> none  [gather_packed(): lines, at, done = (lax.all_gather(vector, axis), 0, [])]
  transfers between devices with their start and end apart: 3 -> 0, of which waited for: 2 -> 0; matrix products, arithmetic and copies ran while one was open for 15% -> 0% of each run, Pallas kernels for 0% -> 0%
where the time goes in v1:
time: 103 us
  Pallas kernels  100 us (97%)
  local copies, waits for them, and re-layouts  2.32 us (2%)
    pallas_call x1, Pallas kernels, shards(): pl.pallas_call(body, out_shape=(jax.ShapeDtypeStruct((1, TOK), F32), jax....  100 us

profile of v1, /device:TPU:1, one launch (start us, length us, event | category | flops | bytes accessed | tf_op | source)
XLA Modules:
  0.0 103.0 jit_solution(17811033528156056231)
XLA Ops:
  0.6 100.0 %kl_all.1 = (f32[1,128]{1,0:T(1,128)}, f32[8,128]{1,0:T(8,128)}) custom-call(bf16[128,512]{1,0:T(8,128)(2,1)} %th.1, bf16[128,128]{1,0:T(8,128)(2,1)} %sh.1, bf16[2048,2048]{1,0:T(8,128)(2,1)} %tw.1, bf16[4,128,2048]{2,1,0:T(8,128)(2,1)} %bitcast.3), custom_call_target="tpu_custom_call" | custom-call | tf_op jit(solution)/shard_map/kl_all/pallas_call | solution.py:415
  100.7 1.2 %slice.3 = f32[1,1]{1,0:T(1,128)} slice(f32[8,128]{1,0:T(8,128)} %get-tuple-element.5), slice={[0:1], [0:1]} | slice | bytes 8 | tf_op jit(solution)/shard_map/slice | solution.py:447
  101.9 1.1 %copy.7 = f32[128]{0:T(128)} copy(f32[128]{0:T(128)} %bitcast.4) | data formatting | bytes 1024

commit v2 on v1

v2 whole, which is shorter than its diff:
```python
import math

import jax
import jax.numpy as jnp
from jax import lax
from jax.experimental import pallas as pl
from jax.experimental.pallas import tpu as pltpu
from jax.sharding import PartitionSpec as P

NX, NY, NZ = 4, 4, 8
TOK = 128
HALF = TOK // 2
TF = 512
SF = 128
VB = 2048
CB = VB // NY
F32 = jnp.float32

OWN, LEFT, RIGHT, OPP = (0, 64), (128, 256), (192, 320), (384, 448)
N_STAGES = 4
AR = 384
BR = 4 * TOK - AR
N_SEND, N_RECV = 15, 74


def body(
    th, sh, tw, sw,
    kl_ref, loss_ref,
    tst, tbuf, sbuf, twb, swb, swst, pbuf, ropp, rfin, slog, stat, st1, st3, st4, kl_v, loss_v,
    ssem, rsem, lsem,
):
    dp = lax.axis_index("dp")
    v = lax.axis_index("vocab")
    y, c = lax.div(dp, 2), lax.rem(dp, 2)
    x, z = lax.div(v, NZ), lax.rem(v, NZ)
    o = 1 - c

    def dev(xx, yy, zz, cc):
        return (yy * 2 + cc, xx * NZ + zz)

    def xm(d):
        return lax.rem(x + (d + NX), NX)

    def ym(d):
        return lax.rem(y + (d + NY), NY)

    def zm(d):
        return lax.rem(z + (d + NZ), NZ)

    R, L = dev(xm(1), y, z, c), dev(xm(-1), y, z, c)
    U, D = dev(x, ym(1), z, c), dev(x, ym(-1), z, c)
    F, B = dev(x, y, zm(1), c), dev(x, y, zm(-1), c)
    mate = dev(x, y, z, o)

    s_index, r_index = {}, {}
    s_bytes, r_bytes = {}, {}

    def nbytes(ref):
        return math.prod(ref.shape) * jnp.dtype(ref.dtype).itemsize

    def remote(src, dst, device, sgroup, rgroup):
        i = s_index.setdefault(sgroup, len(s_index))
        j = r_index.setdefault(rgroup, len(r_index))
        s_bytes[sgroup] = s_bytes.get(sgroup, 0) + nbytes(src)
        r_bytes[rgroup] = r_bytes.get(rgroup, 0) + nbytes(dst)
        return pltpu.make_async_remote_copy(
            src_ref=src,
            dst_ref=dst,
            send_sem=ssem.at[i],
            recv_sem=rsem.at[j],
            device_id=device,
            device_id_type=pl.DeviceIdType.MESH,
        )

    def send(src, dst, device, sgroup, rgroup):
        remote(src, dst, device, sgroup, rgroup).start()

    def awaiting(ref, i, j):
        return pltpu.make_async_remote_copy(
            src_ref=ref,
            dst_ref=ref,
            send_sem=ssem.at[i],
            recv_sem=rsem.at[j],
            device_id=mate,
            device_id_type=pl.DeviceIdType.MESH,
        )

    def arrived(rgroup, ref):
        assert r_bytes.pop(rgroup) == nbytes(ref), rgroup
        awaiting(ref, 0, r_index[rgroup]).wait_recv()

    def sent(sgroup, ref):
        assert s_bytes.pop(sgroup) == nbytes(ref), sgroup
        awaiting(ref, s_index[sgroup], 0).wait_send()

    th_in = pltpu.make_async_copy(th, tst, lsem.at[4])
    th_in.start()
    sh_here = sbuf.at[z, pl.ds(y * TOK, TOK), pl.ds(x * SF, SF)]
    sh_own = pltpu.make_async_copy(sh, sh_here, lsem.at[2])
    sh_own.start()

    def tshard(row, zz, n=HALF):
        return tbuf.at[pl.ds(row, n), pl.ds(zz * TF, TF)]

    stays = jnp.logical_and(c == 0, x == y)
    moves = jnp.logical_or(c == 1, x != y)
    th_own = pltpu.make_async_copy(th, tshard(0, z, TOK), lsem.at[3])

    @pl.when(stays)
    def _():
        th_own.start()

    tw_own = pltpu.make_async_copy(tw, twb.at[pl.ds(c * VB, VB), :], lsem.at[0])
    tw_own.start()
    sw_own = pltpu.make_async_copy(
        sw.at[:, :, pl.ds(y * CB, CB)], swb.at[pl.ds(c * 4, 4), pl.ds(y * SF, SF), :], lsem.at[1]
    )
    sw_own.start()

    barrier = pltpu.get_barrier_semaphore()
    peers = [dev(xm(d), y, z, c) for d in (1, -1)]
    peers += [dev(x, ym(d), z, c) for d in (1, -1, 2)]
    peers += [dev(x, y, zm(d), c) for d in (1, -1)]
    peers += [mate]
    for p in peers:
        pl.semaphore_signal(barrier, inc=1, device_id=p, device_id_type=pl.DeviceIdType.MESH)

    @pl.when(moves)
    def _():
        source = dev(y, lax.rem(x + 2 * c, NY), z, c)
        pl.semaphore_signal(barrier, inc=1, device_id=source, device_id_type=pl.DeviceIdType.MESH)
        pl.semaphore_wait(barrier, len(peers) + 1)

    @pl.when(stays)
    def _():
        pl.semaphore_wait(barrier, len(peers))

    th_in.wait()
    sh_own.wait()
    th_move = remote(tst, tshard(0, z, TOK), dev(lax.rem(y + 2 * c, NX), x, z, c), "th", "th")

    @pl.when(moves)
    def _():
        th_move.start()

    for d in (1, -1, 2):
        send(sh_here, sh_here, dev(x, ym(d), z, c), "sy", "sy")

    opp = ym(2)
    send(sw.at[pl.ds(0, 2), :, pl.ds(opp * CB, CB)], swst.at[0], D, "sw", "swst0")
    send(sw.at[pl.ds(2, 2), :, pl.ds(opp * CB, CB)], swst.at[1], U, "sw", "swst1")

    def sw_rows(src, first, n):
        return swb.at[pl.ds(c * 4 + first, n), pl.ds(src * SF, SF), :]

    send(sw.at[:, :, pl.ds(ym(1) * CB, CB)], sw_rows(y, 0, 4), U, "sw", "sw_u")
    send(sw.at[:, :, pl.ds(ym(-1) * CB, CB)], sw_rows(y, 0, 4), D, "sw", "sw_d")

    def forward_sw():
        arrived("swst0", swst.at[0])
        send(swst.at[0], sw_rows(ym(1), 0, 2), D, "sw", "swf")
        arrived("swst1", swst.at[1])
        send(swst.at[1], sw_rows(ym(-1), 2, 2), U, "sw", "swf")

    for k in range(4):
        send(tw.at[pl.ds(k * 512, 512), :], twb.at[pl.ds(c * VB + k * 512, 512), :], mate, "tw", "tw")

    @pl.when(moves)
    def _():
        th_move.wait_recv()

    @pl.when(stays)
    def _():
        th_own.wait()

    def tz_send(way, off, h):
        part = tshard(HALF * h, zm(off))
        send(part, part, F if way == "f" else B, "tz", ("tz", way, abs(off) + 1, h))

    def tz_arrived(way, k, h):
        arrived(("tz", way, k, h), tshard(HALF * h, z))

    def tx_first(off):
        zz = zm(off)
        send(tshard(OWN[0], zz), tshard(LEFT[0], zz), R, "tx", "L0")
        send(tshard(OWN[0], zz), tshard(RIGHT[0], zz), L, "tx", "R0")

    def rows64(row, part=None):
        cols = pl.ds(0, NZ * TF) if part is None else pl.ds(part * 4 * TF, 4 * TF)
        return tbuf.at[pl.ds(row, HALF), cols]

    for h in (0, 1):
        tz_send("f", 0, h)
        tz_send("b", 0, h)

    def sx_rows(xx, lo=0, n=AR):
        return sbuf.at[z, pl.ds(lo, n), pl.ds(xx * SF, SF)]

    arrived("sy", sbuf.at[0, pl.ds(0, 3 * TOK), pl.ds(0, SF)])
    send(sx_rows(x), sx_rows(x), R, "sx", "sxr")
    send(sx_rows(x), sx_rows(x), L, "sx", "sxl")
    tx_first(0)

    def forward_sx():
        h = AR // 2
        arrived("sxr", sx_rows(x))
        send(sx_rows(xm(-1), 0, h), sx_rows(xm(-1), 0, h), R, "sx", "sxfr")
        arrived("sxl", sx_rows(x))
        send(sx_rows(xm(1), h, h), sx_rows(xm(1), h, h), L, "sx", "sxfl")

    for k in (1, 2, 3):
        for h in (0, 1):
            tz_arrived("f", k, h)
            if k < 3 or h == 0:
                tz_send("f", -k, h)
            tz_arrived("b", k, h)
            if k < 3 or h == 1:
                tz_send("b", k, h)
        if k == 2:
            forward_sx()
        tx_first(-k)
        tx_first(k)
        if k == 2:
            forward_sw()
    tz_arrived("f", 4, 0)
    tx_first(4)
    tz_arrived("b", 4, 1)
    for part in (0, 1):
        send(rows64(OWN[1], part), rows64(LEFT[1], part), R, "tx", "L1")
        send(rows64(OWN[1], part), rows64(RIGHT[1], part), L, "tx", ("R1", part))

    def sz_send(way, off, h):
        part = sbuf.at[zm(off), pl.ds(AR // 2 * h, AR // 2), :]
        send(part, part, F if way == "f" else B, "sz", ("sz", way, abs(off) + 1, h))

    def sz_arrived(way, k, h):
        arrived(("sz", way, k, h), sbuf.at[z, pl.ds(0, AR // 2), :])

    def sz_step(k, h):
        sz_arrived("f", k, h)
        if k < 3 or h == 0:
            sz_send("f", -k, h)
        sz_arrived("b", k, h)
        if k < 3 or h == 1:
            sz_send("b", k, h)

    def sb_send(way, off, lo=AR, n=BR):
        part = sbuf.at[zm(off), pl.ds(lo, n), pl.ds(x * SF, SF)]
        send(part, part, F if way == "f" else B, "sb", ("sb", way, abs(off) + 1))

    def sb_step(k):
        for way, sign, lo in (("f", -1, AR), ("b", 1, AR + BR // 2)):
            arrived(("sb", way, k), sbuf.at[z, pl.ds(AR, BR), pl.ds(0, SF)])
            sb_send(way, sign * k) if k < 3 else sb_send(way, sign * k, lo, BR // 2)

    def sb_rows(xx, z0=0, nz=NZ):
        return sbuf.at[pl.ds(z0, nz), pl.ds(AR, BR), pl.ds(xx * SF, SF)]

    def sbx_send():
        for way in ("f", "b"):
            arrived(("sb", way, 4), sbuf.at[z, pl.ds(AR, BR // 2), pl.ds(0, SF)])
        send(sb_rows(x), sb_rows(x), R, "sbx", "sbr")
        send(sb_rows(x), sb_rows(x), L, "sbx", "sbl")

    def forward_sbx():
        arrived("sbr", sb_rows(x))
        send(sb_rows(xm(-1), 0, 4), sb_rows(xm(-1), 0, 4), R, "sbx", "sbf")
        arrived("sbl", sb_rows(x))
        send(sb_rows(xm(1), 4, 4), sb_rows(xm(1), 4, 4), L, "sbx", "sbf")

    def start_sz():
        sb_send("f", 0)
        sb_send("b", 0)
        arrived("sxfr", sx_rows(x, 0, AR // 2))
        sz_send("f", 0, 0)
        sz_send("b", 0, 0)
        arrived("sxfl", sx_rows(x, 0, AR // 2))
        sz_send("f", 0, 1)
        sz_send("b", 0, 1)

    def product(stage, q0, q1):
        lo = stage * TOK

        def step(i, carry):
            q = lax.div(i, 2)
            h = lax.rem(i, 2)
            tgt = lax.rem(y + jnp.where(q == 0, 2, jnp.where(q == 1, 3, jnp.where(q == 2, 1, 0))), NY)
            cols = pl.ds(pl.multiple_of(tgt * CB + h * 256, 256), 256)
            pbuf[q, lo : lo + TOK, pl.ds(pl.multiple_of(h * 256, 256), 256)] = jnp.dot(
                tbuf[lo : lo + TOK, :], twb[:, cols], preferred_element_type=F32
            )
            return carry

        lax.fori_loop(2 * q0, 2 * q1, step, 0)

    def halves(stage):
        return pl.ds(stage * TOK, HALF), pl.ds(stage * TOK + HALF, HALF)

    def send_opp(stage):
        a, b = halves(stage)
        send(pbuf.at[0, a, :], ropp.at[a, :], D, "rs", ("oa", stage))
        send(pbuf.at[0, b, :], ropp.at[b, :], U, "rs", ("ob", stage))

    def send_plain(stage):
        a, b = halves(stage)
        send(pbuf.at[1, b, :], rfin.at[0, b, :], D, "rs", ("fin", stage))
        send(pbuf.at[2, a, :], rfin.at[1, a, :], U, "rs", ("fin", stage))

    def send_sums(stage):
        a, b = halves(stage)
        lo = stage * TOK
        mid, hi = lo + HALF, lo + TOK
        arrived(("oa", stage), ropp.at[a, :])
        pbuf[1, lo:mid, :] += ropp[lo:mid, :]
        send(pbuf.at[1, a, :], rfin.at[0, a, :], D, "rs", ("fin", stage))
        arrived(("ob", stage), ropp.at[b, :])
        pbuf[2, mid:hi, :] += ropp[mid:hi, :]
        send(pbuf.at[2, b, :], rfin.at[1, b, :], U, "rs", ("fin", stage))

    def teacher_stage(stage, between):
        product(stage, 0, 1)
        send_opp(stage)
        between()
        product(stage, 1, 4)
        send_plain(stage)

    def to_mate(src):
        send(sw_rows(src, 0, 4), sw_rows(src, 0, 4), mate, "mate", "mate")

    def student(first, last, lo=0, n=AR):
        def step(i, carry):
            zz = lax.rem(z + i, NZ)
            slog[lo : lo + n, :] += jnp.dot(
                sbuf[zz, lo : lo + n, :], swb[zz], preferred_element_type=F32
            )
            return carry

        lax.fori_loop(first, last, step, 0)

    tw_own.wait()
    arrived("tw", twb.at[pl.ds(0, VB), :])
    teacher_stage(0, start_sz)

    arrived("L0", rows64(LEFT[0]))
    send(rows64(LEFT[0]), rows64(OPP[0]), R, "tx", "O0")
    arrived("R0", rows64(RIGHT[0]))

    def stage_one():
        send_sums(0)
        sb_step(1)

    teacher_stage(1, stage_one)

    sw_own.wait()
    to_mate(y)
    arrived("sw_u", sw_rows(y, 0, 4))
    to_mate(ym(-1))
    arrived("sw_d", sw_rows(y, 0, 4))
    to_mate(ym(1))

    sz_step(1, 0)
    sb_step(2)
    send_sums(1)
    sz_step(1, 1)
    for part in (0, 1):
        arrived(("R1", part), rows64(RIGHT[1], 0))
        send(rows64(RIGHT[1], part), rows64(OPP[1], part), L, "tx", "O1")
    arrived("L1", rows64(LEFT[1]))
    teacher_stage(2, lambda: sb_step(3))
    arrived("swf", sw_rows(y, 0, 4))
    to_mate(ym(2))
    sz_step(2, 0)
    send_sums(2)
    sz_step(2, 1)
    sbx_send()
    arrived("O0", rows64(OPP[0]))
    arrived("O1", rows64(OPP[1]))
    teacher_stage(3, lambda: sz_step(3, 0))
    slog[...] = jnp.zeros_like(slog)
    arrived("mate", swb.at[pl.ds(0, 4)])
    student(6, 11)
    sz_step(3, 1)
    forward_sbx()
    send_sums(3)
    student(5, 6)
    student(3, 4)
    sz_arrived("f", 4, 0)
    sz_arrived("b", 4, 1)
    student(4, 5)
    arrived("sbf", sb_rows(x))
    student(0, NZ, AR, BR)

    sent("sy", sbuf.at[0, pl.ds(0, 3 * TOK), pl.ds(0, SF)])
    sent("sx", sbuf.at[0, pl.ds(0, 288), :])
    sent("tz", tbuf.at[pl.ds(0, 112), :])
    sent("tx", tbuf.at[pl.ds(0, 384), :])
    sent("sz", sbuf.at[pl.ds(0, 7), pl.ds(0, AR), :])
    sent("sb", sbuf.at[0, pl.ds(0, 224), :])
    sent("sbx", sbuf.at[pl.ds(0, 2), pl.ds(0, 384), :])
    sent("sw", swb.at[pl.ds(0, 4)])
    sent("mate", swb.at[pl.ds(0, 4)])
    sent("tw", twb.at[pl.ds(0, VB), :])

    @pl.when(moves)
    def _():
        th_move.wait_send()

    lane = lax.broadcasted_iota(jnp.int32, (TOK, 128), 1)

    def token_stats(first_rows, ahead):
        group = lax.rem(x + 2 * c + ahead, NY)

        def rows(ref, *at):
            return jnp.concatenate([ref[(*at, slice(r, r + HALF))] for r in first_rows], axis=0)

        t = rows(pbuf, 3) + rows(rfin, 0) + rows(rfin, 1)
        s = slog[pl.ds(pl.multiple_of(group * TOK, TOK), TOK), :]
        t_top = jnp.max(t, axis=1, keepdims=True)
        s_top = jnp.max(s, axis=1, keepdims=True)
        e = jnp.exp(t - t_top)
        t_sum = jnp.sum(e, axis=1, keepdims=True)
        w = jnp.sum(e * (t - s), axis=1, keepdims=True)
        s_sum = jnp.sum(jnp.exp(s - s_top), axis=1, keepdims=True)
        both = jnp.where(
            lane == 0, t_top,
            jnp.where(lane == 1, t_sum, jnp.where(lane == 2, w, jnp.where(lane == 3, s_top, s_sum))),
        )
        stat[group] = jnp.transpose(both)[:8, :]

    def stage_done(stage):
        arrived(("fin", stage), rfin.at[0, pl.ds(0, 2 * TOK), :])

    stage_done(0)
    token_stats(OWN, 0)
    stage_done(1)
    stage_done(2)
    token_stats(LEFT, 3)
    token_stats(RIGHT, 1)
    stage_done(3)
    token_stats(OPP, 2)

    def merged(ref, n):
        parts = [ref[k] for k in range(n)]
        t_top = parts[0][0:1]
        s_top = parts[0][3:4]
        for p in parts[1:]:
            t_top = jnp.maximum(t_top, p[0:1])
            s_top = jnp.maximum(s_top, p[3:4])
        t_sum = w = s_sum = jnp.zeros((1, 128), F32)
        for p in parts:
            a = jnp.exp(p[0:1] - t_top)
            b = jnp.exp(p[3:4] - s_top)
            t_sum += p[1:2] * a
            w += p[2:3] * a
            s_sum += p[4:5] * b
        return t_top, t_sum, w, s_top, s_sum

    def put(ref, k, rows):
        zero = jnp.zeros((3, 128), F32)
        ref[k] = jnp.concatenate([*rows, zero], axis=0)

    me = x * NY + y
    st1[me] = stat[y]
    for dy in range(NY):
        for dx in range(NX):
            if dx or dy:
                send(stat.at[ym(dy)], st1.at[me], dev(xm(dx), ym(dy), z, c), "st1", "st1")
    sent("rs", pbuf.at[pl.ds(0, 3)])
    arrived("st1", st1.at[pl.ds(0, NX * NY - 1)])
    put(st3, z, merged(st1, NX * NY))
    for d in range(1, NZ):
        send(st3.at[z], st3.at[z], dev(x, y, zm(d), c), "st3", "st3")
    sent("st1", st1.at[pl.ds(0, NX * NY - 1)])
    arrived("st3", st3.at[pl.ds(0, NZ - 1)])
    t_top, t_sum, w, s_top, s_sum = merged(st3, NZ)
    kl = w / t_sum - (t_top + jnp.log(t_sum)) + (s_top + jnp.log(s_sum))
    st4[dp] = jnp.broadcast_to(jnp.sum(kl, axis=1, keepdims=True), (8, 128))
    for d in range(1, 8):
        send(st4.at[dp], st4.at[dp], (lax.rem(dp + d, 8), v), "st4", "st4")
    kl_v[...] = kl
    kl_out = pltpu.make_async_copy(kl_v, kl_ref, lsem.at[5])
    kl_out.start()
    sent("st3", st3.at[pl.ds(0, NZ - 1)])
    arrived("st4", st4.at[pl.ds(0, 7)])
    total = st4[0]
    for k in range(1, 8):
        total += st4[k]
    loss_v[...] = total[0:1] * (1.0 / (TOK * 8))
    loss_out = pltpu.make_async_copy(loss_v, loss_ref, lsem.at[6])
    loss_out.start()
    sent("st4", st4.at[pl.ds(0, 7)])
    kl_out.wait()
    loss_out.wait()
    assert set(s_bytes) == {"th"} and set(r_bytes) == {"th"}, (s_bytes, r_bytes)
    assert (len(s_index), len(r_index)) == (N_SEND, N_RECV), (len(s_index), len(r_index))


def shards(th, sh, tw, sw):
    hbm = pl.BlockSpec(memory_space=pl.ANY)
    bf16 = jnp.bfloat16
    kl, loss = pl.pallas_call(
        body,
        out_shape=(
            jax.ShapeDtypeStruct((1, TOK), F32),
            jax.ShapeDtypeStruct((1, 128), F32),
        ),
        in_specs=[hbm] * 4,
        out_specs=(hbm, hbm),
        scratch_shapes=[
            pltpu.VMEM((TOK, TF), bf16),
            pltpu.VMEM((4 * TOK, NZ * TF), bf16),
            pltpu.VMEM((NZ, 4 * TOK, NX * SF), bf16),
            pltpu.VMEM((2 * VB, VB), bf16),
            pltpu.VMEM((NZ, NX * SF, CB), bf16),
            pltpu.VMEM((2, 2, SF, CB), bf16),
            pltpu.VMEM((4, 4 * TOK, CB), F32),
            pltpu.VMEM((4 * TOK, CB), F32),
            pltpu.VMEM((2, 4 * TOK, CB), F32),
            pltpu.VMEM((4 * TOK, CB), F32),
            pltpu.VMEM((NY, 8, 128), F32),
            pltpu.VMEM((NX * NY, 8, 128), F32),
            pltpu.VMEM((NZ, 8, 128), F32),
            pltpu.VMEM((8, 8, 128), F32),
            pltpu.VMEM((1, TOK), F32),
            pltpu.VMEM((1, 128), F32),
            pltpu.SemaphoreType.DMA((N_SEND,)),
            pltpu.SemaphoreType.DMA((N_RECV,)),
            pltpu.SemaphoreType.DMA((7,)),
        ],
        compiler_params=pltpu.CompilerParams(
            collective_id=0, has_side_effects=True, vmem_limit_bytes=60 * 1024 * 1024
        ),
        name="kl_all",
    )(th, sh, tw, sw.reshape(4, SF, VB))
    return (kl.reshape(TOK), loss[0, 0])


def solution(mesh):
    in_specs = (P("dp", "vocab"),) * 4
    return jax.shard_map(
        shards, mesh=mesh, in_specs=in_specs, out_specs=(P("dp"), P()), check_vma=False
    )
```

time: 103 us -> 93.8 us (0.911)
  Pallas kernels: 100 us -> 90.2 us
  between operations: 0.64 us -> 2.4 us
  local copies, waits for them, and re-layouts: 2.32 us -> 1.11 us
    pallas_call x1, Pallas kernels: 100 us -> 90.2 us  [shards(): pl.pallas_call(body, out_shape=(jax.ShapeDtypeStruct((1, TOK), F32), jax....]
    slice x1 -> x0, local copies, waits for them, and re-layouts: 1.18 us -> none  [shards(): return (kl.reshape(TOK), loss[0, 0])]
where the time goes in v2:
time: 93.8 us; the launch traced here: 93.7 us
  Pallas kernels  90.2 us (96%)
  between operations  2.4 us (3%)
  local copies, waits for them, and re-layouts  1.11 us (1%)
    pallas_call x1, Pallas kernels, shards(): pl.pallas_call(body, out_shape=(jax.ShapeDtypeStruct((1, TOK), F32), jax....  90.2 us

profile of v2, /device:TPU:1, one launch (start us, length us, event | category | flops | bytes accessed | tf_op | source)
XLA Modules:
  0.0 93.7 jit_solution(17345854841093021078)
XLA Ops:
  0.6 90.2 %kl_all.1 = (f32[1,128]{1,0:T(1,128)}, f32[1,128]{1,0:T(1,128)}) custom-call(bf16[128,512]{1,0:T(8,128)(2,1)} %th.1, bf16[128,128]{1,0:T(8,128)(2,1)} %sh.1, bf16[2048,2048]{1,0:T(8,128)(2,1)} %tw.1, bf16[4,128,2048]{2,1,0:T(8,128)(2,1)} %bitcast.4), custom_call_target="tpu_custom_call" | custom-call | tf_op jit(solution)/shard_map/kl_all/pallas_call | solution.py:501
  90.9 1.1 %copy.8 = f32[128]{0:T(128)} copy(f32[128]{0:T(128)} %bitcast.6) | data formatting | bytes 1024

commit v3 on v2

--- a/solution.py
+++ b/solution.py
@@ -165,6 +165,30 @@
     for k in range(4):
         send(tw.at[pl.ds(k * 512, 512), :], twb.at[pl.ds(c * VB + k * 512, 512), :], mate, "tw", "tw")
 
+    def sb_send(way, off, lo=AR, n=BR):
+        part = sbuf.at[zm(off), pl.ds(lo, n), pl.ds(x * SF, SF)]
+        send(part, part, F if way == "f" else B, "sb", ("sb", way, abs(off) + 1))
+
+    def sb_step(k):
+        for way, sign, lo in (("f", -1, AR), ("b", 1, AR + BR // 2)):
+            arrived(("sb", way, k), sbuf.at[z, pl.ds(AR, BR), pl.ds(0, SF)])
+            sb_send(way, sign * k) if k < 3 else sb_send(way, sign * k, lo, BR // 2)
+
+    def sb_rows(xx, z0=0, nz=NZ):
+        return sbuf.at[pl.ds(z0, nz), pl.ds(AR, BR), pl.ds(xx * SF, SF)]
+
+    def sbx_send():
+        for way in ("f", "b"):
+            arrived(("sb", way, 4), sbuf.at[z, pl.ds(AR, BR // 2), pl.ds(0, SF)])
+        send(sb_rows(x), sb_rows(x), R, "sbx", "sbr")
+        send(sb_rows(x), sb_rows(x), L, "sbx", "sbl")
+
+    def forward_sbx():
+        arrived("sbr", sb_rows(x))
+        send(sb_rows(xm(-1), 0, 4), sb_rows(xm(-1), 0, 4), R, "sbx", "sbf")
+        arrived("sbl", sb_rows(x))
+        send(sb_rows(xm(1), 4, 4), sb_rows(xm(1), 4, 4), L, "sbx", "sbf")
+
     @pl.when(moves)
     def _():
         th_move.wait_recv()
@@ -197,6 +221,8 @@
         return sbuf.at[z, pl.ds(lo, n), pl.ds(xx * SF, SF)]
 
     arrived("sy", sbuf.at[0, pl.ds(0, 3 * TOK), pl.ds(0, SF)])
+    sb_send("f", 0)
+    sb_send("b", 0)
     send(sx_rows(x), sx_rows(x), R, "sx", "sxr")
     send(sx_rows(x), sx_rows(x), L, "sx", "sxl")
     tx_first(0)
@@ -220,6 +246,7 @@
             forward_sx()
         tx_first(-k)
         tx_first(k)
+        sb_step(k)
         if k == 2:
             forward_sw()
     tz_arrived("f", 4, 0)
@@ -244,33 +271,7 @@
         if k < 3 or h == 1:
             sz_send("b", k, h)
 
-    def sb_send(way, off, lo=AR, n=BR):
-        part = sbuf.at[zm(off), pl.ds(lo, n), pl.ds(x * SF, SF)]
-        send(part, part, F if way == "f" else B, "sb", ("sb", way, abs(off) + 1))
-
-    def sb_step(k):
-        for way, sign, lo in (("f", -1, AR), ("b", 1, AR + BR // 2)):
-            arrived(("sb", way, k), sbuf.at[z, pl.ds(AR, BR), pl.ds(0, SF)])
-            sb_send(way, sign * k) if k < 3 else sb_send(way, sign * k, lo, BR // 2)
-
-    def sb_rows(xx, z0=0, nz=NZ):
-        return sbuf.at[pl.ds(z0, nz), pl.ds(AR, BR), pl.ds(xx * SF, SF)]
-
-    def sbx_send():
-        for way in ("f", "b"):
-            arrived(("sb", way, 4), sbuf.at[z, pl.ds(AR, BR // 2), pl.ds(0, SF)])
-        send(sb_rows(x), sb_rows(x), R, "sbx", "sbr")
-        send(sb_rows(x), sb_rows(x), L, "sbx", "sbl")
-
-    def forward_sbx():
-        arrived("sbr", sb_rows(x))
-        send(sb_rows(xm(-1), 0, 4), sb_rows(xm(-1), 0, 4), R, "sbx", "sbf")
-        arrived("sbl", sb_rows(x))
-        send(sb_rows(xm(1), 4, 4), sb_rows(xm(1), 4, 4), L, "sbx", "sbf")
-
     def start_sz():
-        sb_send("f", 0)
-        sb_send("b", 0)
         arrived("sxfr", sx_rows(x, 0, AR // 2))
         sz_send("f", 0, 0)
         sz_send("b", 0, 0)
@@ -317,13 +318,6 @@
         pbuf[2, mid:hi, :] += ropp[mid:hi, :]
         send(pbuf.at[2, b, :], rfin.at[1, b, :], U, "rs", ("fin", stage))
 
-    def teacher_stage(stage, between):
-        product(stage, 0, 1)
-        send_opp(stage)
-        between()
-        product(stage, 1, 4)
-        send_plain(stage)
-
     def to_mate(src):
         send(sw_rows(src, 0, 4), sw_rows(src, 0, 4), mate, "mate", "mate")
 
@@ -339,17 +333,29 @@
 
     tw_own.wait()
     arrived("tw", twb.at[pl.ds(0, VB), :])
-    teacher_stage(0, start_sz)
+    product(0, 0, 1)
+    send_opp(0)
+    start_sz()
+    product(0, 1, 4)
+    send_plain(0)
 
     arrived("L0", rows64(LEFT[0]))
     send(rows64(LEFT[0]), rows64(OPP[0]), R, "tx", "O0")
     arrived("R0", rows64(RIGHT[0]))
-
-    def stage_one():
-        send_sums(0)
-        sb_step(1)
-
-    teacher_stage(1, stage_one)
+    product(1, 0, 1)
+    send_opp(1)
+    product(1, 1, 2)
+    sz_step(1, 0)
+    product(1, 2, 3)
+
+    def forward_right(part):
+        arrived(("R1", part), rows64(RIGHT[1], 0))
+        send(rows64(RIGHT[1], part), rows64(OPP[1], part), L, "tx", "O1")
+
+    send_sums(0)
+    forward_right(0)
+    product(1, 3, 4)
+    send_plain(1)
 
     sw_own.wait()
     to_mate(y)
@@ -358,27 +364,31 @@
     arrived("sw_d", sw_rows(y, 0, 4))
     to_mate(ym(1))
 
-    sz_step(1, 0)
-    sb_step(2)
+    sz_step(1, 1)
+    forward_right(1)
+    sbx_send()
+    arrived("L1", rows64(LEFT[1]))
+    product(2, 0, 1)
+    send_opp(2)
     send_sums(1)
-    sz_step(1, 1)
-    for part in (0, 1):
-        arrived(("R1", part), rows64(RIGHT[1], 0))
-        send(rows64(RIGHT[1], part), rows64(OPP[1], part), L, "tx", "O1")
-    arrived("L1", rows64(LEFT[1]))
-    teacher_stage(2, lambda: sb_step(3))
+    product(2, 1, 2)
+    sz_step(2, 0)
+    product(2, 2, 4)
+    send_plain(2)
     arrived("swf", sw_rows(y, 0, 4))
     to_mate(ym(2))
-    sz_step(2, 0)
+    sz_step(2, 1)
     send_sums(2)
-    sz_step(2, 1)
-    sbx_send()
-    arrived("O0", rows64(OPP[0]))
-    arrived("O1", rows64(OPP[1]))
-    teacher_stage(3, lambda: sz_step(3, 0))
     slog[...] = jnp.zeros_like(slog)
     arrived("mate", swb.at[pl.ds(0, 4)])
     student(6, 11)
+    arrived("O0", rows64(OPP[0]))
+    arrived("O1", rows64(OPP[1]))
+    product(3, 0, 1)
+    send_opp(3)
+    sz_step(3, 0)
+    product(3, 1, 4)
+    send_plain(3)
     sz_step(3, 1)
     forward_sbx()
     send_sums(3)
@@ -485,7 +495,7 @@
     total = st4[0]
     for k in range(1, 8):
         total += st4[k]
-    loss_v[...] = total[0:1] * (1.0 / (TOK * 8))
+    loss_v[...] = total * (1.0 / (TOK * 8))
     loss_out = pltpu.make_async_copy(loss_v, loss_ref, lsem.at[6])
     loss_out.start()
     sent("st4", st4.at[pl.ds(0, 7)])
@@ -502,7 +512,7 @@
         body,
         out_shape=(
             jax.ShapeDtypeStruct((1, TOK), F32),
-            jax.ShapeDtypeStruct((1, 128), F32),
+            jax.ShapeDtypeStruct((8, 128), F32),
         ),
         in_specs=[hbm] * 4,
         out_specs=(hbm, hbm),
@@ -522,7 +532,7 @@
             pltpu.VMEM((NZ, 8, 128), F32),
             pltpu.VMEM((8, 8, 128), F32),
             pltpu.VMEM((1, TOK), F32),
-            pltpu.VMEM((1, 128), F32),
+            pltpu.VMEM((8, 128), F32),
             pltpu.SemaphoreType.DMA((N_SEND,)),
             pltpu.SemaphoreType.DMA((N_RECV,)),
             pltpu.SemaphoreType.DMA((7,)),

time: 93.8 us -> 89.4 us (0.953)
  Pallas kernels: 90.2 us -> 86.3 us
  between operations: 2.4 us -> 0.64 us
  local copies, waits for them, and re-layouts: 1.11 us -> 2.32 us
    pallas_call x1, Pallas kernels: 90.2 us -> 86.3 us  [shards(): pl.pallas_call(body, out_shape=(jax.ShapeDtypeStruct((1, TOK), F32), jax....]
    slice x0 -> x1, local copies, waits for them, and re-layouts: none -> 1.18 us  [shards(): return (kl.reshape(TOK), loss[0, 0])]
where the time goes in v3:
time: 89.4 us; the launch traced here: 89.3 us
  Pallas kernels  86.3 us (97%)
  local copies, waits for them, and re-layouts  2.32 us (3%)
    pallas_call x1, Pallas kernels, shards(): pl.pallas_call(body, out_shape=(jax.ShapeDtypeStruct((1, TOK), F32), jax....  86.3 us

profile of v3, /device:TPU:1, one launch (start us, length us, event | category | flops | bytes accessed | tf_op | source)
XLA Modules:
  0.0 89.3 jit_solution(4914850825769612797)
XLA Ops:
  0.6 86.3 %kl_all.1 = (f32[1,128]{1,0:T(1,128)}, f32[8,128]{1,0:T(8,128)}) custom-call(bf16[128,512]{1,0:T(8,128)(2,1)} %th.1, bf16[128,128]{1,0:T(8,128)(2,1)} %sh.1, bf16[2048,2048]{1,0:T(8,128)(2,1)} %tw.1, bf16[4,128,2048]{2,1,0:T(8,128)(2,1)} %bitcast.3), custom_call_target="tpu_custom_call" | custom-call | tf_op jit(solution)/shard_map/kl_all/pallas_call | solution.py:511
  86.9 1.2 %slice.3 = f32[1,1]{1,0:T(1,128)} slice(f32[8,128]{1,0:T(8,128)} %get-tuple-element.5), slice={[0:1], [0:1]} | slice | bytes 8 | tf_op jit(solution)/shard_map/slice | solution.py:545
  88.1 1.1 %copy.7 = f32[128]{0:T(128)} copy(f32[128]{0:T(128)} %bitcast.4) | data formatting | bytes 1024

commit v4 on v3

--- a/solution.py
+++ b/solution.py
@@ -26,7 +26,7 @@
 def body(
     th, sh, tw, sw,
     kl_ref, loss_ref,
-    tst, tbuf, sbuf, twb, swb, swst, pbuf, ropp, rfin, slog, stat, st1, st3, st4, kl_v, loss_v,
+    tst, tbuf, sbuf, twb, swb, swst, pbuf, ropp, rfin, slog, stat, st1, st3, st4,
     ssem, rsem, lsem,
 ):
     dp = lax.axis_index("dp")
@@ -394,11 +394,11 @@
     send_sums(3)
     student(5, 6)
     student(3, 4)
+    arrived("sbf", sb_rows(x))
+    student(0, NZ, AR, BR)
     sz_arrived("f", 4, 0)
     sz_arrived("b", 4, 1)
     student(4, 5)
-    arrived("sbf", sb_rows(x))
-    student(0, NZ, AR, BR)
 
     sent("sy", sbuf.at[0, pl.ds(0, 3 * TOK), pl.ds(0, SF)])
     sent("sx", sbuf.at[0, pl.ds(0, 288), :])
@@ -471,51 +471,50 @@
 
     me = x * NY + y
     st1[me] = stat[y]
-    for dy in range(NY):
-        for dx in range(NX):
-            if dx or dy:
-                send(stat.at[ym(dy)], st1.at[me], dev(xm(dx), ym(dy), z, c), "st1", "st1")
+    far = (2, 1, 3, 0)
+    for dx, dy in sorted(((dx, dy) for dx in far for dy in far), key=lambda d: -sum(min(k, 4 - k) for k in d))[:-1]:
+        send(stat.at[ym(dy)], st1.at[me], dev(xm(dx), ym(dy), z, c), "st1", "st1")
     sent("rs", pbuf.at[pl.ds(0, 3)])
     arrived("st1", st1.at[pl.ds(0, NX * NY - 1)])
     put(st3, z, merged(st1, NX * NY))
-    for d in range(1, NZ):
+    for d in (4, 3, 5, 2, 6, 1, 7):
         send(st3.at[z], st3.at[z], dev(x, y, zm(d), c), "st3", "st3")
     sent("st1", st1.at[pl.ds(0, NX * NY - 1)])
     arrived("st3", st3.at[pl.ds(0, NZ - 1)])
     t_top, t_sum, w, s_top, s_sum = merged(st3, NZ)
     kl = w / t_sum - (t_top + jnp.log(t_sum)) + (s_top + jnp.log(s_sum))
     st4[dp] = jnp.broadcast_to(jnp.sum(kl, axis=1, keepdims=True), (8, 128))
-    for d in range(1, 8):
+    for d in (4, 5, 3, 2, 6, 7, 1):
         send(st4.at[dp], st4.at[dp], (lax.rem(dp + d, 8), v), "st4", "st4")
-    kl_v[...] = kl
-    kl_out = pltpu.make_async_copy(kl_v, kl_ref, lsem.at[5])
-    kl_out.start()
+    kl_ref[...] = kl
     sent("st3", st3.at[pl.ds(0, NZ - 1)])
     arrived("st4", st4.at[pl.ds(0, 7)])
     total = st4[0]
     for k in range(1, 8):
         total += st4[k]
-    loss_v[...] = total * (1.0 / (TOK * 8))
-    loss_out = pltpu.make_async_copy(loss_v, loss_ref, lsem.at[6])
-    loss_out.start()
+    loss_ref[...] = total * (1.0 / (TOK * 8))
     sent("st4", st4.at[pl.ds(0, 7)])
-    kl_out.wait()
-    loss_out.wait()
     assert set(s_bytes) == {"th"} and set(r_bytes) == {"th"}, (s_bytes, r_bytes)
     assert (len(s_index), len(r_index)) == (N_SEND, N_RECV), (len(s_index), len(r_index))
 
 
+def hand_out(kl_in, loss_in, kl_ref, loss_ref):
+    kl_ref[...] = kl_in[...]
+    loss_ref[...] = loss_in[0:1, 0:1]
+
+
 def shards(th, sh, tw, sw):
     hbm = pl.BlockSpec(memory_space=pl.ANY)
+    vmem = pl.BlockSpec(memory_space=pltpu.VMEM)
     bf16 = jnp.bfloat16
     kl, loss = pl.pallas_call(
         body,
         out_shape=(
-            jax.ShapeDtypeStruct((1, TOK), F32),
-            jax.ShapeDtypeStruct((8, 128), F32),
+            pltpu.VMEM((1, TOK), F32),
+            pltpu.VMEM((8, 128), F32),
         ),
         in_specs=[hbm] * 4,
-        out_specs=(hbm, hbm),
+        out_specs=(vmem, vmem),
         scratch_shapes=[
             pltpu.VMEM((TOK, TF), bf16),
             pltpu.VMEM((4 * TOK, NZ * TF), bf16),
@@ -531,18 +530,24 @@
             pltpu.VMEM((NX * NY, 8, 128), F32),
             pltpu.VMEM((NZ, 8, 128), F32),
             pltpu.VMEM((8, 8, 128), F32),
-            pltpu.VMEM((1, TOK), F32),
-            pltpu.VMEM((8, 128), F32),
             pltpu.SemaphoreType.DMA((N_SEND,)),
             pltpu.SemaphoreType.DMA((N_RECV,)),
-            pltpu.SemaphoreType.DMA((7,)),
+            pltpu.SemaphoreType.DMA((5,)),
         ],
         compiler_params=pltpu.CompilerParams(
             collective_id=0, has_side_effects=True, vmem_limit_bytes=60 * 1024 * 1024
         ),
         name="kl_all",
     )(th, sh, tw, sw.reshape(4, SF, VB))
-    return (kl.reshape(TOK), loss[0, 0])
+    vmem = pl.BlockSpec(memory_space=pltpu.VMEM)
+    kl, loss = pl.pallas_call(
+        hand_out,
+        out_shape=(jax.ShapeDtypeStruct((1, TOK), F32), jax.ShapeDtypeStruct((1, 1), F32)),
+        in_specs=[vmem] * 2,
+        out_specs=(vmem, vmem),
+        name="hand_out",
+    )(*(pltpu.with_memory_space_constraint(a, pltpu.VMEM) for a in (kl, loss)))
+    return (kl.reshape(TOK), loss.reshape(()))
 
 
 def solution(mesh):

time: 89.4 us -> 86.3 us (0.965)
  local copies, waits for them, and re-layouts: 2.32 us -> 0 us
    slice x1 -> x0, local copies, waits for them, and re-layouts: 1.18 us -> none  [shards(): return (kl.reshape(TOK), loss[0, 0])]
    unnamed x1 -> x0, local copies, waits for them, and re-layouts: 1.14 us -> none
    pallas_call x1 -> x2, Pallas kernels: 86.3 us -> 85.6 us  [the longest x1 85.1 us: shards(): pl.pallas_call(body, out_shape=(pltpu.VMEM((1, TOK), F32), pltpu.VMEM((8,...]
where the time goes in v4:
time: 86.3 us; the launch traced here: 86.2 us
  Pallas kernels  85.6 us (99%)
    pallas_call x1, Pallas kernels, shards(): pl.pallas_call(body, out_shape=(pltpu.VMEM((1, TOK), F32), pltpu.VMEM((8,...  85.1 us

profile of v4, /device:TPU:1, one launch (start us, length us, event | category | flops | bytes accessed | tf_op | source)
XLA Modules:
  0.0 86.2 jit_solution(17270510523953691082)
XLA Ops:
  0.6 85.1 %kl_all.1 = (f32[1,128]{1,0:T(1,128)S(1)}, f32[8,128]{1,0:T(8,128)S(1)}) custom-call(bf16[128,512]{1,0:T(8,128)(2,1)} %th.1, bf16[128,128]{1,0:T(8,128)(2,1)} %sh.1, bf16[2048,2048]{1,0:T(8,128)(2,1)} %tw.1, bf16[4,128,2048]{2,1,0:T(8,128)(2,1)} %bitcast.3), custom_call_target="tpu_custom_call" | custom-call | tf_op jit(solution)/shard_map/kl_all/pallas_call | solution.py:510
  85.7 0.5 hand_out.1

commit v5 on v4

--- a/solution.py
+++ b/solution.py
@@ -302,10 +302,20 @@
         send(pbuf.at[0, a, :], ropp.at[a, :], D, "rs", ("oa", stage))
         send(pbuf.at[0, b, :], ropp.at[b, :], U, "rs", ("ob", stage))
 
-    def send_plain(stage):
-        a, b = halves(stage)
+    def send_down(stage):
+        b = halves(stage)[1]
         send(pbuf.at[1, b, :], rfin.at[0, b, :], D, "rs", ("fin", stage))
+
+    def send_up(stage):
+        a = halves(stage)[0]
         send(pbuf.at[2, a, :], rfin.at[1, a, :], U, "rs", ("fin", stage))
+
+    def products_left(stage):
+        product(stage, 1, 2)
+        send_down(stage)
+        product(stage, 2, 3)
+        send_up(stage)
+        product(stage, 3, 4)
 
     def send_sums(stage):
         a, b = halves(stage)
@@ -336,8 +346,7 @@
     product(0, 0, 1)
     send_opp(0)
     start_sz()
-    product(0, 1, 4)
-    send_plain(0)
+    products_left(0)
 
     arrived("L0", rows64(LEFT[0]))
     send(rows64(LEFT[0]), rows64(OPP[0]), R, "tx", "O0")
@@ -345,8 +354,10 @@
     product(1, 0, 1)
     send_opp(1)
     product(1, 1, 2)
+    send_down(1)
     sz_step(1, 0)
     product(1, 2, 3)
+    send_up(1)
 
     def forward_right(part):
         arrived(("R1", part), rows64(RIGHT[1], 0))
@@ -355,7 +366,6 @@
     send_sums(0)
     forward_right(0)
     product(1, 3, 4)
-    send_plain(1)
 
     sw_own.wait()
     to_mate(y)
@@ -372,9 +382,11 @@
     send_opp(2)
     send_sums(1)
     product(2, 1, 2)
+    send_down(2)
     sz_step(2, 0)
-    product(2, 2, 4)
-    send_plain(2)
+    product(2, 2, 3)
+    send_up(2)
+    product(2, 3, 4)
     arrived("swf", sw_rows(y, 0, 4))
     to_mate(ym(2))
     sz_step(2, 1)
@@ -387,8 +399,7 @@
     product(3, 0, 1)
     send_opp(3)
     sz_step(3, 0)
-    product(3, 1, 4)
-    send_plain(3)
+    products_left(3)
     sz_step(3, 1)
     forward_sbx()
     send_sums(3)

time: 86.3 us -> 86.3 us (level)
  no operation moved by 1% of the time
where the time goes in v5:
time: 86.3 us; the launch traced here: 86.2 us
  Pallas kernels  85.6 us (99%)
    pallas_call x1, Pallas kernels, shards(): pl.pallas_call(body, out_shape=(pltpu.VMEM((1, TOK), F32), pltpu.VMEM((8,...  85.1 us

profile of v5, /device:TPU:1, one launch (start us, length us, event | category | flops | bytes accessed | tf_op | source)
XLA Modules:
  0.0 86.2 jit_solution(23978488392097865)
XLA Ops:
  0.6 85.1 %kl_all.1 = (f32[1,128]{1,0:T(1,128)S(1)}, f32[8,128]{1,0:T(8,128)S(1)}) custom-call(bf16[128,512]{1,0:T(8,128)(2,1)} %th.1, bf16[128,128]{1,0:T(8,128)(2,1)} %sh.1, bf16[2048,2048]{1,0:T(8,128)(2,1)} %tw.1, bf16[4,128,2048]{2,1,0:T(8,128)(2,1)} %bitcast.3), custom_call_target="tpu_custom_call" | custom-call | tf_op jit(solution)/shard_map/kl_all/pallas_call | solution.py:521
  85.7 0.5 hand_out.1
